TPU v7x, 32 devices: a whole 2x2x4 slice. The times are simulated.
32 devices in a mesh: section: 4 (over z), fsdp: 4 (over y, core), tp: 2 (over x).
Axes of the slice: x: 2, y: 2, z: 4, core: 2. Of those that a mesh axis runs over, the one named last changes fastest.
Arguments:
- stash: bfloat16 [4, 4, 512, 2304], P('section', None, 'fsdp'), may hold values from -6 to 6
- grad_now: bfloat16 [4, 512, 2304], P('section', 'fsdp'), may hold values from -6 to 6
- grad_top: bfloat16 [2, 512, 2304], P(None, 'fsdp'), may hold values from -6 to 6
- order: int32 [4, 4], P('section'), may hold values from 0 to 3, each once within a row
- gain: float32 [4, 2304], P('section'), may hold values from 0.5 to 1.5
- weight: bfloat16 [4, 2304, 2048], P('section', 'fsdp', 'tp'), may hold values from -0.125 to 0.125
Outputs:
- grad_held: bfloat16 [4, 512, 2304], P('section', 'fsdp')
- weight_grad: float32 [4, 2304, 2048], P('section', 'fsdp', 'tp')
Inputs may be any that keep to these rules, and one draw needn't show every extreme that they name: Each row of order names every kept micro-batch once.
All inputs are finite; a program needn't handle non-finite values.
Results may differ from a plain program's by a relative error of at most 0.013.
Values may be sent and summed in bfloat16 or wider, within the bound.
A program may use at most 64 MiB of HBM per device.

v0:
```python
import jax
import jax.numpy as jnp
from jax import lax
from jax.sharding import PartitionSpec as P

norm_eps = 1e-06


def shifted(shard, axis, by):
    length = lax.axis_size(axis)
    pairs = [(i, i + by) for i in range(length) if 0 <= i + by < length]
    return lax.ppermute(shard, axis, pairs)


def gelu_tanh(values):
    return jax.nn.gelu(values, approximate=True)


def per_device(stash, grad_now, grad_top, order, gain, weight):
    full_weight = lax.all_gather(weight[0], "fsdp", axis=0, tiled=True)
    section_gain = gain[0]
    is_last = lax.axis_index("section") == lax.axis_size("section") - 1
    tp_count = lax.axis_size("tp")
    tp_place = lax.axis_index("tp")
    feature_count = stash.shape[-1]
    share_width = feature_count // tp_count
    share_start = tp_place * share_width
    rows_here = grad_now.shape[1]
    grad_in = grad_now[0]
    lhs_parts = []
    rhs_parts = []
    for tick_id in range(grad_top.shape[0]):
        slot_id = order[0, tick_id]
        section_in = lax.dynamic_index_in_dim(stash[0], slot_id, 0, keepdims=False)
        values = section_in.astype(jnp.float32)
        inv_rms = lax.rsqrt(jnp.mean(values * values, axis=-1, keepdims=True) + norm_eps)
        scaled = values * inv_rms
        normed = (scaled * section_gain).astype(jnp.bfloat16)
        stacked = jnp.concatenate([normed, grad_in], axis=0)
        products = jnp.dot(stacked, full_weight, preferred_element_type=jnp.float32)
        hidden = products[:rows_here]
        backed = products[rows_here:]
        activated, pullback = jax.vjp(gelu_tanh, hidden)
        grad_pre = pullback(backed)[0].astype(jnp.bfloat16)
        activated = activated.astype(jnp.bfloat16)
        lhs_parts.append(normed)
        lhs_parts.append(grad_in)
        rhs_parts.append(grad_pre)
        rhs_parts.append(activated)
        partial_dh = lax.dot_general(
            grad_pre, full_weight, (((1,), (1,)), ((), ())), preferred_element_type=jnp.float32
        )
        total_share = lax.psum_scatter(
            partial_dh.astype(jnp.bfloat16), "tp", scatter_dimension=1, tiled=True
        ).astype(jnp.float32)
        scaled_share = lax.dynamic_slice_in_dim(scaled, share_start, share_width, 1)
        gain_share = lax.dynamic_slice_in_dim(section_gain, share_start, share_width, 0)
        grad_share = lax.dynamic_slice_in_dim(grad_in, share_start, share_width, 1)
        gained = gain_share * total_share
        moment_sum = lax.psum(jnp.sum(gained * scaled_share, axis=-1), "tp")
        inner_mean = (moment_sum / feature_count)[:, None]
        out_share = (
            grad_share.astype(jnp.float32) + inv_rms * (gained - scaled_share * inner_mean)
        ).astype(jnp.bfloat16)
        arrived = shifted(out_share, "section", -1)
        top_share = lax.dynamic_slice_in_dim(grad_top[tick_id], share_start, share_width, 1)
        held_share = jnp.where(is_last, top_share, arrived)
        grad_in = lax.all_gather(held_share, "tp", axis=1, tiled=True)
    lhs_all = jnp.concatenate(lhs_parts, axis=0)
    rhs_all = jnp.concatenate(rhs_parts, axis=0)
    weight_grad = lax.psum_scatter(
        lax.dot_general(
            lhs_all, rhs_all, (((0,), (0,)), ((), ())), preferred_element_type=jnp.float32
        ).astype(jnp.bfloat16),
        "fsdp",
        scatter_dimension=0,
        tiled=True,
    ).astype(jnp.float32)
    return (grad_in[None], weight_grad[None])


def solution(mesh):
    return jax.shard_map(
        per_device,
        mesh=mesh,
        in_specs=(
            P("section", None, "fsdp", None),
            P("section", "fsdp", None),
            P(None, "fsdp", None),
            P("section", None),
            P("section", None),
            P("section", "fsdp", "tp"),
        ),
        out_specs=(P("section", "fsdp", None), P("section", "fsdp", "tp")),
        check_vma=False,
    )
```

profile of v0, /device:TPU:0, one launch (start us, length us, event | category | flops | bytes accessed | tf_op | source)
XLA Modules:
  0.0 181.7 jit_solution(16638024135752744247)
XLA Ops:
  7.2 0.7 all-gather.3.cloned.1.call-update
  7.9 1.3 fusion.55
  11.8 0.7 reduce.1
  13.9 1.6 fusion.22
  15.5 2.3 %multiply_convert_fusion = (bf16[128,2304]{1,0:T(8,128)(2,1)}, bf16[128,2304]{1,0:T(8,128)(2,1)S(1)}, f32[128,2304]{1,0:T(8,128)S(1)}, f32[128,2304]{1,0:T(8,128)S(1)}) fusion(f32[2304]{0:T(1024)S(1)} %reduce.1, f32[128]{0:T(128)S(1)} %get-tuple-element.16, bf16[1,4,128,2304]{3,2,1,0:T(8,128)(2,1)} %param.6, s32[]{:T(128)S(6)} %select_n.33, ...), kind=kLoop, calls=%fused_computation.31 | loop fusion | flops 2359296 | bytes 4728840 | tf_op jit(solution)/shard_map/convert_element_type | solution.py:38
  17.7 32.0 %all-gather.3.cloned.1.call-done = bf16[1,2304,1024]{2,1,0:T(8,128)(2,1)} async-done(((bf16[1,576,1024]{2,1,0:T(8,128)(2,1)}), bf16[1,2304,1024]{2,1,0:T(8,128)(2,1)}) %all-gather.3.cloned.1.call-update) | async-done | bytes 4718608 | tf_op jit(solution)/shard_map/all_gather | solution.py:20
  49.7 4.0 %fusion.6 = f32[256,1024]{1,0:T(8,128)S(1)} fusion(bf16[1,2304,1024]{2,1,0:T(8,128)(2,1)} %all-gather.3.cloned.1.call-done, bf16[128,2304]{1,0:T(8,128)(2,1)} %bitcast.52, bf16[128,2304]{1,0:T(8,128)(2,1)S(1)} %get-tuple-element.5), kind=kOutput, calls=%fused_computation.7 | convolution fusion | flops 1210318848 | bytes 6946816 | tf_op jit(solution)/shard_map/dot_general | solution.py:40
  53.8 1.1 multiply_convert_fusion.3
  54.9 1.7 fusion.8
  56.5 1.1 copy.8
  57.7 15.4 %reduce-scatter.10.cloned.1.call-done = bf16[1152,128]{1,0:T(8,128)(2,1)} async-done(((bf16[2304,128]{1,0:T(8,128)(2,1)}), bf16[1152,128]{1,0:T(8,128)(2,1)}) %reduce-scatter.10.cloned.1.call-update) | async-done | bytes 294928
  73.1 1.2 copy.9
  74.5 4.9 %psum.14 = f32[128]{0:T(128)S(1)} all-reduce(f32[128]{0:T(128)S(1)} %multiply_reduce_fusion.1), channel_id=1, replica_groups=mesh['section'=4,'fsdp'=4,'tp'=2] {'tp'}, use_global_device_ids=true, to_apply=%region_3.4 | all-reduce | flops 128 | bytes 1024 | tf_op jit(solution)/shard_map/psum | solution.py:60
  79.4 1.3 fusion.36
  80.7 1.4 collective-permute-start
  82.2 8.0 %collective-permute-done = bf16[128,1152]{1,0:T(8,128)(2,1)} collective-permute-done((bf16[128,1152]{1,0:T(8,128)(2,1)S(1)}, bf16[128,1152]{1,0:T(8,128)(2,1)}, u32[]{:S(2)}, u32[]{:S(2)}) %collective-permute-start) | collective-permute-done | bytes 294944 | tf_op jit(solution)/shard_map/ppermute | solution.py:12
  90.2 1.0 bitcast_select_fusion
  91.3 7.5 %all_gather.10 = bf16[128,2304]{1,0:T(8,128)(2,1)S(1)} all-gather(bf16[128,1152]{1,0:T(8,128)(2,1)S(1)} %bitcast_select_fusion), channel_id=1, replica_groups=mesh['section'=4,'fsdp'=4,'tp'=2] {'tp'}, dimensions={1}, use_global_device_ids=true | all-gather | bytes 884736 | tf_op jit(solution)/shard_map/all_gather | solution.py:68
  98.8 3.8 %fusion.2 = f32[256,1024]{1,0:T(8,128)S(1)} fusion(bf16[1,2304,1024]{2,1,0:T(8,128)(2,1)} %all-gather.3.cloned.1.call-done, bf16[128,2304]{1,0:T(8,128)(2,1)S(1)} %all_gather.10, bf16[128,2304]{1,0:T(8,128)(2,1)S(1)} %copy-done.2), kind=kOutput, calls=%fused_computation.3 | convolution fusion | flops 1210318848 | bytes 6946816 | tf_op jit(solution)/shard_map/dot_general | solution.py:40
  102.6 1.1 multiply_convert_fusion.2
  103.7 1.7 fusion.11
  105.3 1.1 copy.10
  106.5 6.3 %convolution_convert_fusion = bf16[2304,1024]{1,0:T(8,128)(2,1)} fusion(bf16[128,2304]{1,0:T(8,128)(2,1)S(1)} %all_gather.10, bf16[128,2304]{1,0:T(8,128)(2,1)} %get-tuple-element.4, bf16[128,2304]{1,0:T(8,128)(2,1)} %bitcast.53, bf16[128,2304]{1,0:T(8,128)(2,1)} %copy-done.3, bf16[128,1024]{1,0:T(8,128)(2,1)} %get-tuple-element.12, ...), kind=kOutput, calls=%fused_computation | convolution fusion | flops 2431909888 | bytes 8126464 | tf_op jit(solution)/shard_map/dot_general | solution.py:72
  112.8 8.2 %reduce-scatter.12.cloned.1.call-done = bf16[1152,128]{1,0:T(8,128)(2,1)} async-done(((bf16[2304,128]{1,0:T(8,128)(2,1)}), bf16[1152,128]{1,0:T(8,128)(2,1)}) %reduce-scatter.12.cloned.1.call-update) | async-done | bytes 294928
  121.0 1.2 copy.11
  122.3 4.9 %psum.15 = f32[128]{0:T(128)S(1)} all-reduce(f32[128]{0:T(128)S(1)} %multiply_reduce_fusion), channel_id=1, replica_groups=mesh['section'=4,'fsdp'=4,'tp'=2] {'tp'}, use_global_device_ids=true, to_apply=%region_7.8 | all-reduce | flops 128 | bytes 1024 | tf_op jit(solution)/shard_map/psum | solution.py:60
  127.5 1.3 collective-permute-start.1
  128.8 8.0 %collective-permute-done.1 = bf16[128,1152]{1,0:T(8,128)(2,1)S(1)} collective-permute-done((bf16[128,1152]{1,0:T(8,128)(2,1)S(1)}, bf16[128,1152]{1,0:T(8,128)(2,1)S(1)}, u32[]{:S(2)}, u32[]{:S(2)}) %collective-permute-start.1) | collective-permute-done | bytes 294944 | tf_op jit(solution)/shard_map/ppermute | solution.py:12
  136.9 7.4 %all_gather.11 = bf16[128,2304]{1,0:T(8,128)(2,1)S(1)} all-gather(bf16[128,1152]{1,0:T(8,128)(2,1)S(1)} %bitcast_select_fusion.1), channel_id=1, replica_groups=mesh['section'=4,'fsdp'=4,'tp'=2] {'tp'}, dimensions={1}, use_global_device_ids=true | all-gather | bytes 884736 | tf_op jit(solution)/shard_map/all_gather | solution.py:68
  144.3 27.2 %reduce-scatter.8.cloned.1.call-done = bf16[576,1024]{1,0:T(8,128)(2,1)} async-done(((bf16[2304,1024]{1,0:T(8,128)(2,1)}), bf16[576,1024]{1,0:T(8,128)(2,1)}) %reduce-scatter.8.cloned.1.call-update) | async-done | bytes 1179664 | tf_op jit(solution)/shard_map/reduce_scatter | solution.py:71
  171.4 3.0 %bitcast_convert_fusion = f32[1,576,1024]{2,1,0:T(8,128)} fusion(bf16[576,1024]{1,0:T(8,128)(2,1)} %reduce-scatter.8.cloned.1.call-done), kind=kLoop, calls=%fused_computation.30 | loop fusion | flops 589824 | bytes 3538944 | tf_op jit(solution)/shard_map/broadcast_in_dim | solution.py:79
  174.4 0.8 copy.13
  (31 shorter events, 1.0 us)
Async XLA Ops:
  7.2 42.6 %all-gather.3.cloned.1.call-start = ((), (), s32[]{:S(2)}) async-start(), calls=%async_computation.4 | async-start | bytes 5898240 | tf_op jit(solution)/shard_map/all_gather | solution.py:20
  7.9 65.2 %reduce-scatter.10.cloned.1.call-start = ((), (), s32[]{:S(2)}) async-start(), calls=%async_computation.5 | async-start | bytes 884736
  17.7 36.1 %copy-start.3 = (bf16[128,2304]{1,0:T(8,128)(2,1)}, bf16[128,2304]{1,0:T(8,128)(2,1)S(1)}, u32[]{:S(2)}) copy-start(bf16[128,2304]{1,0:T(8,128)(2,1)S(1)} %get-tuple-element.5) | copy-start | bytes 1769476
  49.7 5.1 %copy-start = (bf16[1,2304,1024]{2,1,0:T(8,128)(2,1)S(1)}, bf16[1,2304,1024]{2,1,0:T(8,128)(2,1)}, u32[]{:S(2)}) copy-start(bf16[1,2304,1024]{2,1,0:T(8,128)(2,1)} %all-gather.3.cloned.1.call-done) | copy-start | bytes 14155780
  54.9 2.8 %copy-start.4 = (f32[1,2304]{1,0:T(1,128)S(1)}, f32[1,2304]{1,0:T(1,128)}, u32[]{:S(2)}) copy-start(f32[1,2304]{1,0:T(1,128)} %param.10) | copy-start | bytes 27652
  57.6 63.4 %reduce-scatter.12.cloned.1.call-start = ((), (), s32[]{:S(2)}) async-start(), calls=%async_computation.6 | async-start | bytes 884736
  79.4 2.7 %copy-start.1 = (bf16[2,128,2304]{2,1,0:T(8,128)(2,1)S(1)}, bf16[2,128,2304]{2,1,0:T(8,128)(2,1)}, u32[]{:S(2)}) copy-start(bf16[2,128,2304]{2,1,0:T(8,128)(2,1)} %param.8) | copy-start | bytes 3538948
  80.7 18.1 %copy-start.2 = (bf16[128,2304]{1,0:T(8,128)(2,1)S(1)}, bf16[128,2304]{1,0:T(8,128)(2,1)}, u32[]{:S(2)}) copy-start(bf16[128,2304]{1,0:T(8,128)(2,1)} %get-tuple-element.4) | copy-start | bytes 1769476
  80.7 9.5 %collective-permute-start = (bf16[128,1152]{1,0:T(8,128)(2,1)S(1)}, bf16[128,1152]{1,0:T(8,128)(2,1)}, u32[]{:S(2)}, u32[]{:S(2)}) collective-permute-start(bf16[128,1152]{1,0:T(8,128)(2,1)S(1)} %fusion.36), channel_id=1, source_target_pairs={{8,0},{16,8},{24,16},{9,1},{17,9},{25,17},{10,2},{18,10},{26,18},{... | collective-permute-start | bytes 884744 | tf_op jit(solution)/shard_map/ppermute | solution.py:12
  91.2 12.4 %slice-start = ((s8[4718592]{0:T(1024)(128)(4,1)}), s8[4194304]{0:T(1024)(128)(4,1)S(1)}, s32[]{:S(2)}) async-start(s8[4718592]{0:T(1024)(128)(4,1)} %bitcast.45), calls=%async_computation.7 | async-start | bytes 8388608
  98.8 4.9 %slice-start.1 = ((s8[4718592]{0:T(1024)(128)(4,1)}), s8[524288]{0:T(1024)(128)(4,1)S(1)}, s32[]{:S(2)}) async-start(s8[4718592]{0:T(1024)(128)(4,1)} %bitcast.45), calls=%async_computation.8 | async-start | bytes 1048576
  106.4 65.0 %reduce-scatter.8.cloned.1.call-start = ((), (), s32[]{:S(2)}) async-start(), calls=%async_computation.3 | async-start | bytes 5898240 | tf_op jit(solution)/shard_map/reduce_scatter | solution.py:71
  127.5 9.3 %collective-permute-start.1 = (bf16[128,1152]{1,0:T(8,128)(2,1)S(1)}, bf16[128,1152]{1,0:T(8,128)(2,1)S(1)}, u32[]{:S(2)}, u32[]{:S(2)}) collective-permute-start(bf16[128,1152]{1,0:T(8,128)(2,1)S(1)} %add_convert_fusion), channel_id=1, source_target_pairs={{8,0},{16,8},{24,16},{9,1},{17,9},{25,17},{10,2},{18,10},{26,18},{... | collective-permute-start | bytes 884744 | tf_op jit(solution)/shard_map/ppermute | solution.py:12
Sparse Core Ops, SparseCore 0:
  9.5 40.1 all-gather.2
  57.7 15.3 reduce-scatter.9
  106.5 14.4 reduce-scatter.11
  123.4 47.9 reduce-scatter.7
where the time goes:
time: 182 us
  waiting for transfers between devices  99.5 us (55%)
  blocking collectives  24.8 us (14%)
  between operations  17.8 us (10%)
  matrix products  17.5 us (10%)
  other arithmetic  12.6 us (7%)
  local copies, waits for them, and re-layouts  6.68 us (4%)
  starting transfers between devices  2.88 us (2%)
    all_gather x1, waiting for transfers between devices, per_device(): full_weight = lax.all_gather(weight[0], 'fsdp', axis=0, tiled=True)  32 us
    reduce_scatter x1, waiting for transfers between devices, per_device(): lax.psum_scatter(lax.dot_general(lhs_all, rhs_all, (((0,), (0,)), ((), ()...  27.2 us
    unnamed x6, waiting for transfers between devices  24.3 us
    ppermute x2, waiting for transfers between devices, shifted(): return lax.ppermute(shard, axis, pairs)  16 us
    all_gather x2, blocking collectives, per_device(): grad_in = lax.all_gather(held_share, 'tp', axis=1, tiled=True)  14.9 us
    psum x2, blocking collectives, per_device(): moment_sum = lax.psum(jnp.sum(gained * scaled_share, axis=-1), 'tp')  9.85 us
    dot_general x2, matrix products, per_device(): products = jnp.dot(stacked, full_weight, preferred_element_type=jnp.float32)  7.83 us
    dot_general x1, matrix products, per_device(): lax.dot_general(lhs_all, rhs_all, (((0,), (0,)), ((), ())), preferred_ele...  6.34 us
  transfers between devices with their start and end apart: 6, of which 6 were waited for; matrix products, arithmetic and copies ran while one was open for 8% of the time, Pallas kernels for 0%

commit v1 on v0

--- a/solution.py
+++ b/solution.py
@@ -57,7 +57,7 @@
         gain_share = lax.dynamic_slice_in_dim(section_gain, share_start, share_width, 0)
         grad_share = lax.dynamic_slice_in_dim(grad_in, share_start, share_width, 1)
         gained = gain_share * total_share
-        moment_sum = lax.psum(jnp.sum(gained * scaled_share, axis=-1), "tp")
+        moment_sum = jnp.sum(lax.all_gather(jnp.sum(gained * scaled_share, axis=-1), "tp"), axis=0)
         inner_mean = (moment_sum / feature_count)[:, None]
         out_share = (
             grad_share.astype(jnp.float32) + inv_rms * (gained - scaled_share * inner_mean)

time: 182 us -> 182 us (level)
    psum x2 -> x0, blocking collectives: 9.85 us -> none  [per_device(): moment_sum = lax.psum(jnp.sum(gained * scaled_share, axis=-1), 'tp')]
    all_gather x0 -> x2, blocking collectives: none -> 8.46 us  [per_device(): lax.all_gather(jnp.sum(gained * scaled_share, axis=-1), 'tp')]
where the time goes in v1:
time: 182 us; the launch traced here: 181 us
  waiting for transfers between devices  100 us (55%)
  blocking collectives  23.4 us (13%)
  between operations  17.8 us (10%)
  matrix products  17.5 us (10%)
  other arithmetic  12.6 us (7%)
  local copies, waits for them, and re-layouts  6.68 us (4%)
  starting transfers between devices  2.88 us (2%)
    all_gather x1, waiting for transfers between devices, per_device(): full_weight = lax.all_gather(weight[0], 'fsdp', axis=0, tiled=True)  32 us
    reduce_scatter x1, waiting for transfers between devices, per_device(): lax.psum_scatter(lax.dot_general(lhs_all, rhs_all, (((0,), (0,)), ((), ()...  27.8 us
    unnamed x6, waiting for transfers between devices  24.3 us
    ppermute x2, waiting for transfers between devices, shifted(): return lax.ppermute(shard, axis, pairs)  16 us
    all_gather x2, blocking collectives, per_device(): grad_in = lax.all_gather(held_share, 'tp', axis=1, tiled=True)  14.9 us
    all_gather x2, blocking collectives, per_device(): lax.all_gather(jnp.sum(gained * scaled_share, axis=-1), 'tp')  8.46 us
    dot_general x2, matrix products, per_device(): products = jnp.dot(stacked, full_weight, preferred_element_type=jnp.float32)  7.83 us
    dot_general x1, matrix products, per_device(): lax.dot_general(lhs_all, rhs_all, (((0,), (0,)), ((), ())), preferred_ele...  6.34 us
  transfers between devices with their start and end apart: 6, of which 6 were waited for; matrix products, arithmetic and copies ran while one was open for 8% of the time, Pallas kernels for 0%

profile of v1, /device:TPU:0, one launch (start us, length us, event | category | flops | bytes accessed | tf_op | source)
XLA Modules:
  0.0 181.0 jit_solution(15712405206883271262)
XLA Ops:
  7.2 0.7 all-gather.7.cloned.1.call-update
  7.9 1.3 fusion.55
  11.8 0.7 reduce.3
  13.9 1.6 fusion.22
  15.5 2.3 %multiply_convert_fusion = (bf16[128,2304]{1,0:T(8,128)(2,1)}, bf16[128,2304]{1,0:T(8,128)(2,1)S(1)}, f32[128,2304]{1,0:T(8,128)S(1)}, f32[128,2304]{1,0:T(8,128)S(1)}) fusion(f32[2304]{0:T(1024)S(1)} %reduce.3, f32[128]{0:T(128)S(1)} %get-tuple-element.16, bf16[1,4,128,2304]{3,2,1,0:T(8,128)(2,1)} %param.6, s32[]{:T(128)S(6)} %select_n.33, ...), kind=kLoop, calls=%fused_computation.31 | loop fusion | flops 2359296 | bytes 4728840 | tf_op jit(solution)/shard_map/convert_element_type | solution.py:38
  17.7 32.0 %all-gather.7.cloned.1.call-done = bf16[1,2304,1024]{2,1,0:T(8,128)(2,1)} async-done(((bf16[1,576,1024]{2,1,0:T(8,128)(2,1)}), bf16[1,2304,1024]{2,1,0:T(8,128)(2,1)}) %all-gather.7.cloned.1.call-update) | async-done | bytes 4718608 | tf_op jit(solution)/shard_map/all_gather | solution.py:20
  49.7 4.0 %fusion.6 = f32[256,1024]{1,0:T(8,128)S(1)} fusion(bf16[1,2304,1024]{2,1,0:T(8,128)(2,1)} %all-gather.7.cloned.1.call-done, bf16[128,2304]{1,0:T(8,128)(2,1)} %bitcast.54, bf16[128,2304]{1,0:T(8,128)(2,1)S(1)} %get-tuple-element.5), kind=kOutput, calls=%fused_computation.7 | convolution fusion | flops 1210318848 | bytes 6946816 | tf_op jit(solution)/shard_map/dot_general | solution.py:40
  53.8 1.1 multiply_convert_fusion.3
  54.9 1.7 fusion.8
  56.5 1.1 copy.8
  57.7 15.4 %reduce-scatter.10.cloned.1.call-done = bf16[1152,128]{1,0:T(8,128)(2,1)} async-done(((bf16[2304,128]{1,0:T(8,128)(2,1)}), bf16[1152,128]{1,0:T(8,128)(2,1)}) %reduce-scatter.10.cloned.1.call-update) | async-done | bytes 294928
  73.1 1.2 copy.9
  74.5 4.2 %all-gather.3 = f32[2,1,128]{2,1,0:T(1,128)S(1)} all-gather(f32[1,1,128]{2,1,0:T(1,128)S(1)} %bitcast.56), channel_id=3, replica_groups=mesh['section'=4,'fsdp'=4,'tp'=2] {'tp'}, dimensions={0}, use_global_device_ids=true | all-gather | bytes 1536 | tf_op jit(solution)/shard_map/all_gather | solution.py:60
  78.7 1.3 fusion.36
  80.0 1.4 collective-permute-start
  81.5 8.0 %collective-permute-done = bf16[128,1152]{1,0:T(8,128)(2,1)} collective-permute-done((bf16[128,1152]{1,0:T(8,128)(2,1)S(1)}, bf16[128,1152]{1,0:T(8,128)(2,1)}, u32[]{:S(2)}, u32[]{:S(2)}) %collective-permute-start) | collective-permute-done | bytes 294944 | tf_op jit(solution)/shard_map/ppermute | solution.py:12
  89.5 1.0 bitcast_select_fusion
  90.6 7.5 %all_gather.24 = bf16[128,2304]{1,0:T(8,128)(2,1)S(1)} all-gather(bf16[128,1152]{1,0:T(8,128)(2,1)S(1)} %bitcast_select_fusion), channel_id=1, replica_groups=mesh['section'=4,'fsdp'=4,'tp'=2] {'tp'}, dimensions={1}, use_global_device_ids=true | all-gather | bytes 884736 | tf_op jit(solution)/shard_map/all_gather | solution.py:68
  98.1 3.8 %fusion.2 = f32[256,1024]{1,0:T(8,128)S(1)} fusion(bf16[1,2304,1024]{2,1,0:T(8,128)(2,1)} %all-gather.7.cloned.1.call-done, bf16[128,2304]{1,0:T(8,128)(2,1)S(1)} %all_gather.24, bf16[128,2304]{1,0:T(8,128)(2,1)S(1)} %copy-done.2), kind=kOutput, calls=%fused_computation.3 | convolution fusion | flops 1210318848 | bytes 6946816 | tf_op jit(solution)/shard_map/dot_general | solution.py:40
  101.9 1.1 multiply_convert_fusion.2
  103.0 1.7 fusion.11
  104.7 1.1 copy.10
  105.8 6.3 %convolution_convert_fusion = bf16[2304,1024]{1,0:T(8,128)(2,1)} fusion(bf16[128,2304]{1,0:T(8,128)(2,1)S(1)} %all_gather.24, bf16[128,2304]{1,0:T(8,128)(2,1)} %get-tuple-element.4, bf16[128,2304]{1,0:T(8,128)(2,1)} %bitcast.55, bf16[128,2304]{1,0:T(8,128)(2,1)} %copy-done.3, bf16[128,1024]{1,0:T(8,128)(2,1)} %get-tuple-element.12, ...), kind=kOutput, calls=%fused_computation | convolution fusion | flops 2431909888 | bytes 8126464 | tf_op jit(solution)/shard_map/dot_general | solution.py:72
  112.2 8.2 %reduce-scatter.12.cloned.1.call-done = bf16[1152,128]{1,0:T(8,128)(2,1)} async-done(((bf16[2304,128]{1,0:T(8,128)(2,1)}), bf16[1152,128]{1,0:T(8,128)(2,1)}) %reduce-scatter.12.cloned.1.call-update) | async-done | bytes 294928
  120.4 1.2 copy.11
  121.7 4.2 %all-gather.4 = f32[2,1,128]{2,1,0:T(1,128)S(1)} all-gather(f32[1,1,128]{2,1,0:T(1,128)S(1)} %bitcast.57), channel_id=4, replica_groups=mesh['section'=4,'fsdp'=4,'tp'=2] {'tp'}, dimensions={0}, use_global_device_ids=true | all-gather | bytes 1536 | tf_op jit(solution)/shard_map/all_gather | solution.py:60
  126.1 1.3 collective-permute-start.1
  127.4 8.0 %collective-permute-done.1 = bf16[128,1152]{1,0:T(8,128)(2,1)S(1)} collective-permute-done((bf16[128,1152]{1,0:T(8,128)(2,1)S(1)}, bf16[128,1152]{1,0:T(8,128)(2,1)S(1)}, u32[]{:S(2)}, u32[]{:S(2)}) %collective-permute-start.1) | collective-permute-done | bytes 294944 | tf_op jit(solution)/shard_map/ppermute | solution.py:12
  135.5 7.4 %all_gather.27 = bf16[128,2304]{1,0:T(8,128)(2,1)S(1)} all-gather(bf16[128,1152]{1,0:T(8,128)(2,1)S(1)} %bitcast_select_fusion.1), channel_id=1, replica_groups=mesh['section'=4,'fsdp'=4,'tp'=2] {'tp'}, dimensions={1}, use_global_device_ids=true | all-gather | bytes 884736 | tf_op jit(solution)/shard_map/all_gather | solution.py:68
  142.9 27.8 %reduce-scatter.8.cloned.1.call-done = bf16[576,1024]{1,0:T(8,128)(2,1)} async-done(((bf16[2304,1024]{1,0:T(8,128)(2,1)}), bf16[576,1024]{1,0:T(8,128)(2,1)}) %reduce-scatter.8.cloned.1.call-update) | async-done | bytes 1179664 | tf_op jit(solution)/shard_map/reduce_scatter | solution.py:71
  170.7 3.0 %bitcast_convert_fusion = f32[1,576,1024]{2,1,0:T(8,128)} fusion(bf16[576,1024]{1,0:T(8,128)(2,1)} %reduce-scatter.8.cloned.1.call-done), kind=kLoop, calls=%fused_computation.30 | loop fusion | flops 589824 | bytes 3538944 | tf_op jit(solution)/shard_map/broadcast_in_dim | solution.py:79
  173.7 0.8 copy.13
  (33 shorter events, 1.0 us)
Async XLA Ops:
  7.2 42.6 %all-gather.7.cloned.1.call-start = ((), (), s32[]{:S(2)}) async-start(), calls=%async_computation.4 | async-start | bytes 5898240 | tf_op jit(solution)/shard_map/all_gather | solution.py:20
  7.9 65.2 %reduce-scatter.10.cloned.1.call-start = ((), (), s32[]{:S(2)}) async-start(), calls=%async_computation.5 | async-start | bytes 884736
  17.7 36.1 %copy-start.3 = (bf16[128,2304]{1,0:T(8,128)(2,1)}, bf16[128,2304]{1,0:T(8,128)(2,1)S(1)}, u32[]{:S(2)}) copy-start(bf16[128,2304]{1,0:T(8,128)(2,1)S(1)} %get-tuple-element.5) | copy-start | bytes 1769476
  49.7 5.1 %copy-start = (bf16[1,2304,1024]{2,1,0:T(8,128)(2,1)S(1)}, bf16[1,2304,1024]{2,1,0:T(8,128)(2,1)}, u32[]{:S(2)}) copy-start(bf16[1,2304,1024]{2,1,0:T(8,128)(2,1)} %all-gather.7.cloned.1.call-done) | copy-start | bytes 14155780
  54.9 2.8 %copy-start.4 = (f32[1,2304]{1,0:T(1,128)S(1)}, f32[1,2304]{1,0:T(1,128)}, u32[]{:S(2)}) copy-start(f32[1,2304]{1,0:T(1,128)} %param.10) | copy-start | bytes 27652
  57.6 62.7 %reduce-scatter.12.cloned.1.call-start = ((), (), s32[]{:S(2)}) async-start(), calls=%async_computation.6 | async-start | bytes 884736
  78.7 2.7 %copy-start.1 = (bf16[2,128,2304]{2,1,0:T(8,128)(2,1)S(1)}, bf16[2,128,2304]{2,1,0:T(8,128)(2,1)}, u32[]{:S(2)}) copy-start(bf16[2,128,2304]{2,1,0:T(8,128)(2,1)} %param.8) | copy-start | bytes 3538948
  80.0 18.1 %copy-start.2 = (bf16[128,2304]{1,0:T(8,128)(2,1)S(1)}, bf16[128,2304]{1,0:T(8,128)(2,1)}, u32[]{:S(2)}) copy-start(bf16[128,2304]{1,0:T(8,128)(2,1)} %get-tuple-element.4) | copy-start | bytes 1769476
  80.0 9.5 %collective-permute-start = (bf16[128,1152]{1,0:T(8,128)(2,1)S(1)}, bf16[128,1152]{1,0:T(8,128)(2,1)}, u32[]{:S(2)}, u32[]{:S(2)}) collective-permute-start(bf16[128,1152]{1,0:T(8,128)(2,1)S(1)} %fusion.36), channel_id=1, source_target_pairs={{8,0},{16,8},{24,16},{9,1},{17,9},{25,17},{10,2},{18,10},{26,18},{... | collective-permute-start | bytes 884744 | tf_op jit(solution)/shard_map/ppermute | solution.py:12
  90.6 12.4 %slice-start = ((s8[4718592]{0:T(1024)(128)(4,1)}), s8[4194304]{0:T(1024)(128)(4,1)S(1)}, s32[]{:S(2)}) async-start(s8[4718592]{0:T(1024)(128)(4,1)} %bitcast.47), calls=%async_computation.7 | async-start | bytes 8388608
  98.1 4.9 %slice-start.1 = ((s8[4718592]{0:T(1024)(128)(4,1)}), s8[524288]{0:T(1024)(128)(4,1)S(1)}, s32[]{:S(2)}) async-start(s8[4718592]{0:T(1024)(128)(4,1)} %bitcast.47), calls=%async_computation.8 | async-start | bytes 1048576
  105.7 65.0 %reduce-scatter.8.cloned.1.call-start = ((), (), s32[]{:S(2)}) async-start(), calls=%async_computation.3 | async-start | bytes 5898240 | tf_op jit(solution)/shard_map/reduce_scatter | solution.py:71
  126.1 9.3 %collective-permute-start.1 = (bf16[128,1152]{1,0:T(8,128)(2,1)S(1)}, bf16[128,1152]{1,0:T(8,128)(2,1)S(1)}, u32[]{:S(2)}, u32[]{:S(2)}) collective-permute-start(bf16[128,1152]{1,0:T(8,128)(2,1)S(1)} %add_convert_fusion), channel_id=1, source_target_pairs={{8,0},{16,8},{24,16},{9,1},{17,9},{25,17},{10,2},{18,10},{26,18},{... | collective-permute-start | bytes 884744 | tf_op jit(solution)/shard_map/ppermute | solution.py:12
Sparse Core Ops, SparseCore 0:
  9.5 40.1 all-gather.6
  57.7 15.3 reduce-scatter.9
  105.9 14.4 reduce-scatter.11
  122.7 47.9 reduce-scatter.7
